TPU v7x, 32 devices: a whole 2x2x4 slice. The times are simulated.
32 devices in a mesh: row: 4 (over z), col: 2 (over y), layer: 4 (over x, core).
Axes of the slice: x: 2, y: 2, z: 4, core: 2. Of those that a mesh axis runs over, the one named last changes fastest.
Arguments:
- tokens: bfloat16 [1280, 6144], P('row', 'layer'), may hold values from -6 to 6
- expert_ids: int32 [1280, 2], replicated, may hold values from 0 to 7, all different within a row; in each aligned block of 1280 rows (0 to 1279, 1280 to 2559, ...) at most 640 rows name the same one
- w_gate: bfloat16 [2, 6144, 8192], P(None, 'layer', ('row', 'col')), may hold values from -0.078125 to 0.078125
- w_up: bfloat16 [2, 6144, 8192], P(None, 'layer', ('row', 'col')), may hold values from -0.078125 to 0.078125
Outputs:
- hidden: bfloat16 [2, 640, 8192], P(None, ('col', 'layer'), 'row')
Inputs may be any that keep to these rules, and one draw needn't show every extreme that they name: `expert_ids`: each token names 2 different experts. No expert is named by more than 640 tokens, a bound that some block reaches.
All inputs are finite; a program needn't handle non-finite values.
Results may differ from a plain program's by a relative error of at most 0.0012.
Values may be sent and summed in bfloat16 or wider, within the bound.
A program may use at most 128 MiB of HBM per device.

v0:
```python
import jax
import jax.numpy as jnp
from jax import lax
from jax.sharding import PartitionSpec as P

SLOTS_DEV = 80


def passed_along(value, axis, steps):
    count = lax.axis_size(axis)
    pairs = [(source, (source + steps) % count) for source in range(count)]
    return lax.ppermute(value, axis, pairs)


def shards(tokens, expert_ids, w_gate, w_up):
    col_count = lax.axis_size("col")
    layer_count = lax.axis_size("layer")
    row_count = lax.axis_size("row")
    col_index = lax.axis_index("col")
    row_index = lax.axis_index("row")
    experts = w_gate.shape[0]
    capacity = SLOTS_DEV * col_count * layer_count
    slot_block = capacity // col_count
    local_rows = tokens.shape[0]
    tok_count = local_rows * row_count
    expert_range = jnp.arange(experts, dtype=jnp.int32)
    member = jnp.any(expert_ids[:, :, None] == expert_range[None, None, :], axis=1).astype(
        jnp.int32
    )
    slot_rank = jnp.cumsum(member, axis=0) - member
    target = jnp.where(member > 0, slot_rank, capacity)
    token_range = jnp.broadcast_to(jnp.arange(tok_count, dtype=jnp.int32)[:, None], target.shape)
    slot_table = (
        jnp.zeros((experts, capacity + 1), jnp.int32)
        .at[expert_range[None, :], target]
        .set(token_range)
    )
    counts = jnp.sum(member, axis=0)
    slot_start = col_index * slot_block
    picked = lax.dynamic_slice_in_dim(slot_table, slot_start, slot_block, 1)
    position = slot_start + jnp.arange(slot_block, dtype=jnp.int32)
    live_mask = position[None, :] < counts[:, None]
    row_start = row_index * local_rows
    local_pick = picked - row_start
    inside = live_mask & (local_pick >= 0) & (local_pick < local_rows)
    own_rows = tokens[jnp.clip(local_pick, 0, local_rows - 1)]
    placed = jnp.where(inside[:, :, None], own_rows, jnp.zeros((), tokens.dtype)).astype(
        jnp.float32
    )
    slot_rows = lax.psum(placed.astype(jnp.bfloat16), "row")
    stacked = jnp.stack((w_gate, w_up))
    narrow = w_gate.shape[2]
    totals = jnp.zeros((2, experts, slot_block, narrow * col_count), jnp.float32)
    moving = stacked
    for step in range(col_count):
        which_block = (col_index - step) % col_count
        totals = lax.dynamic_update_slice_in_dim(
            totals,
            jnp.einsum("ecd,pedf->pecf", slot_rows, moving, preferred_element_type=jnp.float32),
            which_block * narrow,
            3,
        )
        if step + 1 < col_count:
            moving = passed_along(moving, "col", 1)
    parts = lax.psum_scatter(totals, "layer", scatter_dimension=2, tiled=True)
    return (jax.nn.silu(parts[0]) * parts[1]).astype(jnp.bfloat16)


def solution(mesh):
    in_specs = (
        P("row", "layer"),
        P(),
        P(None, "layer", ("row", "col")),
        P(None, "layer", ("row", "col")),
    )
    out_specs = P(None, ("col", "layer"), "row")
    return jax.shard_map(shards, mesh=mesh, in_specs=in_specs, out_specs=out_specs, check_vma=False)
```

profile of v0, /device:TPU:0, one launch (start us, length us, event | category | flops | bytes accessed | tf_op | source)
XLA Modules:
  0.0 396.8 jit_solution(5306595772369583344)
XLA Ops:
  6.6 10.5 %pad_maximum_fusion = bf16[2,2,1536,1024]{3,2,0,1:T(8,128)(2,1)} fusion(bf16[1,2,1536,1024]{3,2,0,1:T(8,128)(2,1)} %bitcast.45, bf16[1,2,1536,1024]{3,2,0,1:T(8,128)(2,1)} %bitcast.47), kind=kLoop, calls=%fused_computation.2 | loop fusion | flops 6291456 | bytes 25165824 | tf_op jit(solution)/shard_map/stack | solution.py:51
  17.0 3.0 collective-permute-start
  20.1 0.6 reduce-window.6
  20.7 0.2 slice_reduce_fusion
  20.9 0.2 reduce-window.9
  21.1 0.1 convert_reduce_fusion
  21.3 0.1 multiply_reduce_fusion
  21.4 0.1 and_reduce_fusion
  21.5 0.3 copy.15
  21.8 0.3 reshape.36
  22.1 0.3 reshape.38
  22.5 9.9 %scatter_custom_fusion = s32[1282]{0:T(1024)S(1)} fusion(s32[2560]{0:T(1024)S(1)} %reshape.36, s32[2560]{0:T(1024)S(1)} %reshape.38, s32[]{:T(128)} %constant.28.clone.1), kind=kCustom, calls=%fused_computation.31 | custom fusion | bytes 5132
  32.6 3.1 gather_fusion
  35.7 0.1 compare_and_fusion
  35.8 1.6 broadcast_select_fusion
  37.5 82.2 %all-reduce.2.cloned.1.call-done = bf16[2,320,1536]{2,1,0:T(8,128)(2,1)} async-done(((bf16[2,320,1536]{2,1,0:T(8,128)(2,1)}), bf16[2,320,1536]{2,1,0:T(8,128)(2,1)}) %all-reduce.2.cloned.1.call-update) | async-done | bytes 1966096 | tf_op jit(solution)/shard_map/psum | solution.py:50
  119.7 7.9 %convolution_bitcast_fusion.1 = f32[2,2,320,1024]{3,2,0,1:T(8,128)S(1)} fusion(bf16[2,320,1536]{2,1,0:T(8,128)(2,1)} %all-reduce.2.cloned.1.call-done, bf16[1,2,1536,1024]{3,2,0,1:T(8,128)(2,1)} %bitcast.46, bf16[1,2,1536,1024]{3,2,0,1:T(8,128)(2,1)} %bitcast.48), kind=kOutput, calls=%fused_computation.6 | convolution fusion | flops 4051697664 | bytes 19791872 | tf_op jit(solution)/shard_map/ecd,pedf->pecf/dot_general | solution.py:59
  127.6 5.2 %broadcast_in_dim.45 = f32[2,2,320,2048]{3,2,1,0:T(8,128)} broadcast(f32[]{:T(128)} %constant.20.clone.1), dimensions={} | broadcast | bytes 10485764 | tf_op jit(solution)/shard_map/broadcast_in_dim | solution.py:53
  132.8 2.7 copy_dynamic-update-slice_fusion.1
  135.5 155.2 %collective-permute-done = bf16[2,2,1536,1024]{3,2,0,1:T(8,128)(2,1)} collective-permute-done((bf16[2,2,1536,1024]{3,2,0,1:T(8,128)(2,1)}, bf16[2,2,1536,1024]{3,2,0,1:T(8,128)(2,1)}, u32[]{:S(2)}, u32[]{:S(2)}) %collective-permute-start) | collective-permute-done | bytes 12582944 | tf_op jit(solution)/shard_map/ppermute | solution.py:12
  290.7 7.4 %convolution_bitcast_fusion = f32[2,2,320,1024]{3,2,0,1:T(8,128)S(1)} fusion(bf16[2,2,1536,1024]{3,2,0,1:T(8,128)(2,1)} %collective-permute-done, bf16[2,320,1536]{2,1,0:T(8,128)(2,1)S(1)} %copy-done.5), kind=kOutput, calls=%fused_computation.5 | convolution fusion | flops 4026531840 | bytes 19791872 | tf_op jit(solution)/shard_map/ecd,pedf->pecf/dot_general | solution.py:59
  298.1 3.0 copy_dynamic-update-slice_fusion
  301.1 86.0 %reduce-scatter.2.cloned.1.call-done = f32[2,2,80,2048]{3,2,1,0:T(8,128)} async-done(((f32[2,2,320,2048]{3,2,1,0:T(8,128)}), f32[2,2,80,2048]{3,2,1,0:T(8,128)}) %reduce-scatter.2.cloned.1.call-update) | async-done | bytes 2621456 | tf_op jit(solution)/shard_map/reduce_scatter | solution.py:65
  387.1 2.9 fusion.3
  (28 shorter events, 0.5 us)
Async XLA Ops:
  6.5 26.1 %copy-start = (bf16[320,1536]{1,0:T(8,128)(2,1)S(1)}, bf16[320,1536]{1,0:T(8,128)(2,1)}, u32[]{:S(2)}) copy-start(bf16[320,1536]{1,0:T(8,128)(2,1)} %param.4) | copy-start | bytes 2949124
  6.5 113.2 %all-reduce.2.cloned.1.call-start = ((), (), s32[]{:S(2)}) async-start(), calls=%async_computation.1 | async-start | bytes 3932160 | tf_op jit(solution)/shard_map/psum | solution.py:50
  6.5 13.5 %copy-start.2 = (s32[1280,2]{0,1:T(2,128)S(1)}, s32[1280,2]{0,1:T(2,128)}, u32[]{:S(2)}) copy-start(s32[1280,2]{0,1:T(2,128)} %param.5) | copy-start | bytes 30724
  6.5 14.7 %copy-start.3 = (s32[2]{0:T(128)S(1)}, s32[2]{0:T(128)}, u32[]{:S(2)}) copy-start(s32[2]{0:T(128)} %constant.63) | copy-start | bytes 28
  6.5 14.8 %copy-start.4 = (s32[2]{0:T(128)S(1)}, s32[2]{0:T(128)}, u32[]{:S(2)}) copy-start(s32[2]{0:T(128)} %constant.66) | copy-start | bytes 28
  17.0 273.6 %collective-permute-start = (bf16[2,2,1536,1024]{3,2,0,1:T(8,128)(2,1)}, bf16[2,2,1536,1024]{3,2,0,1:T(8,128)(2,1)}, u32[]{:S(2)}, u32[]{:S(2)}) collective-permute-start(bf16[2,2,1536,1024]{3,2,0,1:T(8,128)(2,1)} %pad_maximum_fusion), channel_id=1, source_target_pairs={{0,4},{4,0},{1,5},{5,1},{2,6},{6,2},{3,7},{7,3},{8,12},{12,8},{9,1... | collective-permute-start | bytes 37748744 | tf_op jit(solution)/shard_map/ppermute | solution.py:12
  37.4 349.6 %reduce-scatter.2.cloned.1.call-start = ((), (), s32[]{:S(2)}) async-start(), calls=%async_computation.2 | async-start | bytes 13107200 | tf_op jit(solution)/shard_map/reduce_scatter | solution.py:65
  132.8 157.9 %copy-start.5 = (bf16[2,320,1536]{2,1,0:T(8,128)(2,1)S(1)}, bf16[2,320,1536]{2,1,0:T(8,128)(2,1)}, u32[]{:S(2)}) copy-start(bf16[2,320,1536]{2,1,0:T(8,128)(2,1)} %all-reduce.2.cloned.1.call-done) | copy-start | bytes 5898244
  301.1 88.9 %copy-start.1 = (bf16[320,1536]{1,0:T(8,128)(2,1)S(1)}, bf16[320,1536]{1,0:T(8,128)(2,1)}, u32[]{:S(2)}) copy-start(bf16[320,1536]{1,0:T(8,128)(2,1)} %param.4) | copy-start | bytes 2949124
Sparse Core Ops, SparseCore 0:
  37.5 82.1 all-reduce.1
  301.2 85.7 reduce-scatter.1
where the time goes:
time: 397 us
  waiting for transfers between devices  323 us (81%)
  local copies, waits for them, and re-layouts  25.2 us (6%)
  other arithmetic  16.3 us (4%)
  matrix products  15.3 us (4%)
  between operations  13.6 us (3%)
    ppermute x1, waiting for transfers between devices, passed_along(): return lax.ppermute(value, axis, pairs)  155 us
    reduce_scatter x1, waiting for transfers between devices, shards(): parts = lax.psum_scatter(totals, 'layer', scatter_dimension=2, tiled=True)  86 us
    psum x1, waiting for transfers between devices, shards(): slot_rows = lax.psum(placed.astype(jnp.bfloat16), 'row')  82.2 us
    dot_general x2, matrix products, shards(): jnp.einsum('ecd,pedf->pecf', slot_rows, moving, preferred_element_type=jn...  15.3 us
    unnamed x15, local copies, waits for them, and re-layouts  10.5 us
    another operation x1, other arithmetic, shards(): stacked = jnp.stack((w_gate, w_up))  10.5 us
  transfers between devices with their start and end apart: 3, of which 3 were waited for; matrix products, arithmetic and copies ran while one was open for 8% of the time, Pallas kernels for 0%

commit v1 on v0

v1 whole, which is shorter than its diff:
```python
import functools

import jax
import jax.numpy as jnp
from jax import lax
from jax.experimental import pallas as pl
from jax.experimental.pallas import tpu as pltpu
from jax.sharding import PartitionSpec as P

SLOTS_DEV = 80
CHUNK = 256
PIECE = 512
MESH = pl.DeviceIdType.MESH
VMEM_LIMIT = 62 * 1024 * 1024


def slot_places(expert_ids, experts):
    expert_range = jnp.arange(experts, dtype=jnp.int32)
    member = jnp.any(expert_ids[:, :, None] == expert_range[None, None, :], axis=1).astype(
        jnp.int32
    )
    return member, jnp.cumsum(member, axis=0) - member


def plain_shards(tokens, expert_ids, w_gate, w_up):
    col_count = lax.axis_size("col")
    layer_count = lax.axis_size("layer")
    experts, _, narrow = w_gate.shape
    capacity = SLOTS_DEV * col_count * layer_count
    member, slot_rank = slot_places(expert_ids, experts)
    tok_count = expert_ids.shape[0]
    target = jnp.where(member > 0, slot_rank, capacity)
    everyone = lax.all_gather(tokens, "row", axis=0, tiled=True)
    expert_range = jnp.arange(experts, dtype=jnp.int32)
    token_range = jnp.broadcast_to(jnp.arange(tok_count, dtype=jnp.int32)[:, None], target.shape)
    slot_table = (
        jnp.zeros((experts, capacity + 1), jnp.int32)
        .at[expert_range[None, :], target]
        .set(token_range)
    )[:, :capacity]
    live = jnp.arange(capacity, dtype=jnp.int32)[None, :] < jnp.sum(member, axis=0)[:, None]
    by_layer = (experts, col_count, layer_count, SLOTS_DEV)
    slot_table = slot_table.reshape(by_layer).swapaxes(1, 2).reshape(experts, capacity)
    live = live.reshape(by_layer).swapaxes(1, 2).reshape(experts, capacity)
    slot_rows = jnp.where(live[:, :, None], everyone[slot_table], jnp.zeros((), tokens.dtype))
    totals = jnp.stack(
        [
            jnp.einsum("ecd,edf->ecf", slot_rows, w, preferred_element_type=jnp.float32)
            for w in (w_gate, w_up)
        ]
    )
    parts = lax.psum_scatter(totals, "layer", scatter_dimension=2, tiled=True)
    hidden = (jax.nn.silu(parts[0]) * parts[1]).astype(jnp.bfloat16)
    hidden = hidden.reshape(experts, col_count, SLOTS_DEV, narrow)
    return lax.all_to_all(hidden, "col", 1, 3, tiled=True).reshape(
        experts, SLOTS_DEV, col_count * narrow
    )


def kernel(
    n_row,
    tok_ref,
    tgt_ref,
    wg_hbm,
    wu_hbm,
    out_ref,
    gath,
    wg,
    wu,
    slots,
    keep,
    dsend,
    drecv,
    xsend,
    xrecv,
    ysend,
    yrecv,
    w_sem,
    zs_sem,
    zr_sem,
    fs_sem,
    fr_sem,
    ds_sem,
    dr_sem,
    xs_sem,
    xr_sem,
    ys_sem,
    yr_sem,
):
    experts, depth, narrow = wg.shape
    half = slots.shape[2]
    quarter = tok_ref.shape[1]
    pieces = depth // PIECE
    per_expert = narrow // CHUNK
    chunks = experts * per_expert
    row = lax.axis_index("row")
    col = lax.axis_index("col")
    layer = lax.axis_index("layer")
    core = lax.rem(layer, 2)
    place = lax.div(layer, 2)
    right, left = lax.rem(row + 1, n_row), lax.rem(row + n_row - 1, n_row)
    other_col = {"col": 1 - col}
    other_core = {"layer": layer + 1 - 2 * core}
    other_place = {"layer": lax.rem(layer + 2, 4)}

    w_copies = [
        pltpu.make_async_copy(wg_hbm, wg, w_sem.at[0]),
        pltpu.make_async_copy(wu_hbm, wu, w_sem.at[1]),
    ]
    for copy in w_copies:
        copy.start()

    barrier = pltpu.get_barrier_semaphore()
    for who in ({"row": right}, {"row": left}, other_col, other_core, other_place):
        pl.semaphore_signal(barrier, inc=1, device_id=who, device_id_type=MESH)
    pl.semaphore_wait(barrier, 5)

    def block_of(way, step):
        return lax.rem(row + n_row - step, n_row) if way == 0 else lax.rem(row + step, n_row)

    def ring(way, step, j):
        block = block_of(way, step - 1)
        mine = 2 * way + col
        cols = pl.ds(j * PIECE, PIECE)
        at = gath.at[block, mine, :, cols]
        return pltpu.make_async_remote_copy(
            src_ref=tok_ref.at[mine, :, cols] if step == 1 else at,
            dst_ref=at,
            send_sem=zs_sem.at[way, step - 1, j],
            recv_sem=zr_sem.at[way, step - 1, j],
            device_id={"row": right if way == 0 else left},
            device_id_type=MESH,
        )

    def across(way, step, j):
        at = gath.at[block_of(way, step), 2 * way + col, :, pl.ds(j * PIECE, PIECE)]
        return pltpu.make_async_remote_copy(
            src_ref=at,
            dst_ref=at,
            send_sem=fs_sem.at[way, step - 1, j],
            recv_sem=fr_sem.at[way, step - 1, j],
            device_id=other_col,
            device_id_type=MESH,
        )

    def place_rows(ref, block, way, first):
        rows = ref[pl.ds(2 * way, 2)].reshape(2 * quarter, depth)

        def body(i, carry):
            expert, side = lax.div(i, 2), lax.rem(i, 2)
            want = tgt_ref[block, way, expert]
            here = lax.broadcasted_iota(jnp.int32, (half, 2 * quarter), 0) + side * half
            pick = jnp.where(here == want, 1.0, 0.0).astype(jnp.bfloat16)
            got = jnp.dot(pick, rows, preferred_element_type=jnp.float32).astype(jnp.bfloat16)
            slots[expert, side] = got if first else slots[expert, side] + got
            return carry

        lax.fori_loop(0, 2 * experts, body, 0)

    for j in range(pieces):
        for way in range(2):
            ring(way, 1, j).start()
    place_rows(tok_ref, row, 0, True)
    place_rows(tok_ref, row, 1, False)

    def settle(step):
        for way in range(2):
            for j in range(pieces):
                across(way, step, j).wait_recv()
            block = block_of(way, step)
            place_rows(gath.at[block], block, way, False)

    for step in range(1, n_row):
        for j in range(pieces):
            for way in range(2):
                ring(way, step, j).wait_recv()
                if step + 1 < n_row:
                    ring(way, step + 1, j).start()
                across(way, step, j).start()
        if step > 1:
            settle(step - 1)
    settle(n_row - 1)

    for copy in w_copies:
        copy.wait()

    def core_copy(i):
        return pltpu.make_async_remote_copy(
            src_ref=dsend.at[i],
            dst_ref=drecv.at[i],
            send_sem=ds_sem.at[i],
            recv_sem=dr_sem.at[i],
            device_id=other_core,
            device_id_type=MESH,
        )

    def place_copy(i):
        return pltpu.make_async_remote_copy(
            src_ref=xsend.at[i],
            dst_ref=xrecv.at[i],
            send_sem=xs_sem.at[i],
            recv_sem=xr_sem.at[i],
            device_id=other_place,
            device_id_type=MESH,
        )

    def col_copy(i):
        return pltpu.make_async_remote_copy(
            src_ref=ysend.at[i],
            dst_ref=yrecv.at[i],
            send_sem=ys_sem.at[i],
            recv_sem=yr_sem.at[i],
            device_id=other_col,
            device_id_type=MESH,
        )

    def multiply(i):
        expert, part = lax.div(i, per_expert), lax.rem(i, per_expert)
        cols = pl.ds(pl.multiple_of(part * CHUNK, CHUNK), CHUNK)
        for side, into in ((1 - core, dsend), (core, keep)):
            rows = slots[expert, side]
            for which, w in enumerate((wg, wu)):
                got = jnp.dot(rows, w[expert, :, cols], preferred_element_type=jnp.float32)
                into[i, which] = got.reshape(2, 2, SLOTS_DEV, CHUNK)
        core_copy(i).start()

    def pass_on(i):
        core_copy(i).wait_recv()
        away = 1 - place
        for which in range(2):
            xsend[i, which] = keep[i, which, away] + drecv[i, which, away]
        place_copy(i).start()

    def first_loop(i, carry):
        multiply(i)

        @pl.when(i > 0)
        def _():
            pass_on(i - 1)

        return carry

    lax.fori_loop(0, chunks, first_loop, 0)
    pass_on(chunks - 1)

    def finished(i, side):
        gate, up = [
            keep[i, which, place, side] + drecv[i, which, place, side] + xrecv[i, which, side]
            for which in range(2)
        ]
        return (gate / (1.0 + jnp.exp(-gate)) * up).astype(jnp.bfloat16)

    def columns(i, of_col):
        start = of_col * narrow + lax.rem(i, per_expert) * CHUNK
        return pl.ds(pl.multiple_of(start, CHUNK), CHUNK)

    def finish(i):
        place_copy(i).wait_recv()
        ysend[i] = finished(i, 1 - col)
        out_ref[lax.div(i, per_expert), :, columns(i, col)] = finished(i, col)
        col_copy(i).start()

    def take(i):
        col_copy(i).wait_recv()
        out_ref[lax.div(i, per_expert), :, columns(i, 1 - col)] = yrecv[i]

    def second_loop(i, carry):
        finish(i)

        @pl.when(i > 0)
        def _():
            take(i - 1)

        return carry

    lax.fori_loop(0, chunks, second_loop, 0)
    take(chunks - 1)

    for step in range(1, n_row):
        for way in range(2):
            for j in range(pieces):
                ring(way, step, j).wait_send()
                across(way, step, j).wait_send()

    def last_loop(i, carry):
        core_copy(i).wait_send()
        place_copy(i).wait_send()
        col_copy(i).wait_send()
        return carry

    lax.fori_loop(0, chunks, last_loop, 0)


def vmem_plan(n_row, tokens, w_gate):
    local_rows, depth = tokens.shape
    experts, _, narrow = w_gate.shape
    capacity = SLOTS_DEV * 8
    chunks = experts * narrow // CHUNK
    bf, f32 = jnp.bfloat16, jnp.float32
    return [
        ((n_row, 4, local_rows // 4, depth), bf),
        (w_gate.shape, bf),
        (w_gate.shape, bf),
        ((experts, 2, capacity // 2, depth), bf),
        ((chunks, 2, 2, 2, SLOTS_DEV, CHUNK), f32),
        ((chunks, 2, 2, 2, SLOTS_DEV, CHUNK), f32),
        ((chunks, 2, 2, 2, SLOTS_DEV, CHUNK), f32),
        ((chunks, 2, 2, SLOTS_DEV, CHUNK), f32),
        ((chunks, 2, 2, SLOTS_DEV, CHUNK), f32),
        ((chunks, SLOTS_DEV, CHUNK), bf),
        ((chunks, SLOTS_DEV, CHUNK), bf),
    ]


def fits(n_row, n_col, n_layer, tokens, w_gate):
    local_rows, depth = tokens.shape
    narrow = w_gate.shape[2]
    if n_col != 2 or n_layer != 4 or n_row < 3:
        return False
    if local_rows % 64 or depth % PIECE or narrow % CHUNK:
        return False
    need = sum(
        functools.reduce(lambda a, b: a * b, shape) * jnp.dtype(kind).itemsize
        for shape, kind in vmem_plan(n_row, tokens, w_gate)
    )
    return need < VMEM_LIMIT - 8 * 1024 * 1024


def fused_shards(tokens, expert_ids, w_gate, w_up):
    n_row = lax.axis_size("row")
    experts, depth, narrow = w_gate.shape
    local_rows = tokens.shape[0]
    quarter = local_rows // 4
    chunks = experts * narrow // CHUNK
    pieces = depth // PIECE
    member, rank = slot_places(expert_ids, experts)
    of_col, of_layer, inner = rank // (4 * SLOTS_DEV), rank // SLOTS_DEV % 4, rank % SLOTS_DEV
    spot = ((of_layer % 2 * 2 + of_layer // 2) * 2 + of_col) * SLOTS_DEV + inner
    target = jnp.where(member > 0, spot, -1)
    target = target.reshape(n_row, 2, 1, 2 * quarter, experts).transpose(0, 1, 4, 2, 3)
    dma = pltpu.SemaphoreType.DMA
    ring_sems = dma((2, n_row - 1, pieces))
    return pl.pallas_call(
        functools.partial(kernel, n_row),
        out_shape=jax.ShapeDtypeStruct((experts, SLOTS_DEV, 2 * narrow), jnp.bfloat16),
        in_specs=[
            pl.BlockSpec(memory_space=pltpu.VMEM),
            pl.BlockSpec(memory_space=pltpu.VMEM),
            pl.BlockSpec(memory_space=pl.ANY),
            pl.BlockSpec(memory_space=pl.ANY),
        ],
        out_specs=pl.BlockSpec(memory_space=pltpu.VMEM),
        scratch_shapes=[
            pltpu.VMEM(shape, kind) for shape, kind in vmem_plan(n_row, tokens, w_gate)
        ]
        + [dma((2,))]
        + [ring_sems] * 4
        + [dma((chunks,))] * 6,
        compiler_params=pltpu.CompilerParams(
            collective_id=0, has_side_effects=True, vmem_limit_bytes=VMEM_LIMIT
        ),
    )(tokens.reshape(4, quarter, depth), target, w_gate, w_up)


def solution(mesh):
    def shards(tokens, expert_ids, w_gate, w_up):
        sizes = [mesh.shape[axis] for axis in ("row", "col", "layer")]
        plan = fused_shards if fits(*sizes, tokens, w_gate) else plain_shards
        return plan(tokens, expert_ids, w_gate, w_up)

    in_specs = (
        P("row", "layer"),
        P(),
        P(None, "layer", ("row", "col")),
        P(None, "layer", ("row", "col")),
    )
    out_specs = P(None, ("col", "layer"), "row")
    return jax.shard_map(shards, mesh=mesh, in_specs=in_specs, out_specs=out_specs, check_vma=False)
```

time: 397 us -> 118 us (0.30)
  waiting for transfers between devices: 323 us -> 0 us
  Pallas kernels: 0 us -> 113 us
  local copies, waits for them, and re-layouts: 25.2 us -> 2.9 us
  matrix products: 15.3 us -> 0 us
  other arithmetic: 16.3 us -> 1.72 us
  between operations: 13.6 us -> 0.04 us
    ppermute x1 -> x0, waiting for transfers between devices: 155 us -> none  [passed_along(): return lax.ppermute(value, axis, pairs)]
    pallas_call x0 -> x1, Pallas kernels: none -> 113 us  [fused_shards(): pl.pallas_call(functools.partial(kernel, n_row), out_shape=jax.ShapeDtype...]
    reduce_scatter x1 -> x0, waiting for transfers between devices: 86 us -> none  [shards(): parts = lax.psum_scatter(totals, 'layer', scatter_dimension=2, tiled=True)]
    psum x1 -> x0, waiting for transfers between devices: 82.2 us -> none  [shards(): slot_rows = lax.psum(placed.astype(jnp.bfloat16), 'row')]
    dot_general x2 -> x0, matrix products: 15.3 us -> none  [shards(): jnp.einsum('ecd,pedf->pecf', slot_rows, moving, preferred_element_type=jn...]
    another operation x4 -> x3, other arithmetic: 11.3 us -> 0.78 us  [the longest x1 10.5 us: shards(): stacked = jnp.stack((w_gate, w_up))]
    unnamed x15 -> x1, local copies, waits for them, and re-layouts: 10.5 us -> 1.98 us
    broadcast_in_dim x5 -> x0, local copies, waits for them, and re-layouts: 5.67 us -> none  [the longest x1 5.21 us: shards(): jnp.zeros((2, experts, slot_block, narrow * col_count), jnp.float32)]
  transfers between devices with their start and end apart: 3 -> 0, of which waited for: 3 -> 0; matrix products, arithmetic and copies ran while one was open for 8% -> 0% of each run, Pallas kernels for 0% -> 0%
where the time goes in v1:
time: 118 us; the launch traced here: 117 us
  Pallas kernels  113 us (96%)
  local copies, waits for them, and re-layouts  2.9 us (2%)
  other arithmetic  1.72 us (1%)
    pallas_call x1, Pallas kernels, fused_shards(): pl.pallas_call(functools.partial(kernel, n_row), out_shape=jax.ShapeDtype...  113 us

profile of v1, /device:TPU:0, one launch (start us, length us, event | category | flops | bytes accessed | tf_op | source)
XLA Modules:
  0.0 117.4 jit_solution(8264505591212042690)
XLA Ops:
  0.0 0.7 compare_reduce_fusion
  0.8 0.6 reduce-window.6
  1.4 0.2 slice_reduce_fusion
  1.5 0.2 reduce-window.9
  1.7 0.1 add_bitcast_fusion
  1.8 0.1 compare_select_fusion.2
  1.9 0.1 reshape.21
  2.0 0.6 copy.14
  2.7 112.8 %shard_map.46 = bf16[2,80,2048]{2,1,0:T(8,128)(2,1)} custom-call(bf16[4,80,1536]{2,1,0:T(8,128)(2,1)} %bitcast.23, s32[4,2,2,1,160]{4,3,2,1,0:T(1,128)} %bitcast.24, bf16[2,1536,1024]{2,1,0:T(8,128)(2,1)} %wg_hbm.1, bf16[2,1536,1024]{2,1,0:T(8,128)(2,1)} %wu_hbm.1), custom_call_target="tpu_custom_call" | custom-call | tf_op jit(solution)/shard_map/pallas_call | solution.py:343
  115.4 2.0 %copy.16 = bf16[2,80,2048]{2,1,0:T(8,128)(2,1)} copy(bf16[2,80,2048]{2,1,0:T(8,128)(2,1)} %shard_map.46) | data formatting | bytes 1310720
  (2 shorter events, 0.0 us)

commit v2 on v1

--- a/solution.py
+++ b/solution.py
@@ -10,6 +10,8 @@
 SLOTS_DEV = 80
 CHUNK = 256
 PIECE = 512
+STEPS = 32767.0
+TINY = 1e-30
 MESH = pl.DeviceIdType.MESH
 VMEM_LIMIT = 62 * 1024 * 1024
 
@@ -73,6 +75,8 @@
     drecv,
     xsend,
     xrecv,
+    unit_out,
+    unit_in,
     ysend,
     yrecv,
     w_sem,
@@ -84,6 +88,8 @@
     dr_sem,
     xs_sem,
     xr_sem,
+    us_sem,
+    ur_sem,
     ys_sem,
     yr_sem,
 ):
@@ -204,6 +210,16 @@
             device_id_type=MESH,
         )
 
+    def unit_copy(i):
+        return pltpu.make_async_remote_copy(
+            src_ref=unit_out.at[i],
+            dst_ref=unit_in.at[i],
+            send_sem=us_sem.at[i],
+            recv_sem=ur_sem.at[i],
+            device_id=other_place,
+            device_id_type=MESH,
+        )
+
     def col_copy(i):
         return pltpu.make_async_remote_copy(
             src_ref=ysend.at[i],
@@ -228,7 +244,15 @@
         core_copy(i).wait_recv()
         away = 1 - place
         for which in range(2):
-            xsend[i, which] = keep[i, which, away] + drecv[i, which, away]
+            total = keep[i, which, away] + drecv[i, which, away]
+            total = total.reshape(2 * SLOTS_DEV // 8, 8, CHUNK)
+            top = jnp.maximum(jnp.max(jnp.abs(total), axis=0), TINY)
+            unit_out[i, which] = top * (1.0 / STEPS)
+            coded = jnp.round(total * (STEPS / top)[None])
+            xsend[i, which] = (
+                coded.reshape(2, SLOTS_DEV, CHUNK).astype(jnp.int32).astype(jnp.int16)
+            )
+        unit_copy(i).start()
         place_copy(i).start()
 
     def first_loop(i, carry):
@@ -244,10 +268,13 @@
     pass_on(chunks - 1)
 
     def finished(i, side):
-        gate, up = [
-            keep[i, which, place, side] + drecv[i, which, place, side] + xrecv[i, which, side]
-            for which in range(2)
-        ]
+        sums = []
+        for which in range(2):
+            far = xrecv[i, which, side].astype(jnp.int32).astype(jnp.float32)
+            far = far.reshape(SLOTS_DEV // 8, 8, CHUNK) * unit_in[i, which][None]
+            near = keep[i, which, place, side] + drecv[i, which, place, side]
+            sums.append(near + far.reshape(SLOTS_DEV, CHUNK))
+        gate, up = sums
         return (gate / (1.0 + jnp.exp(-gate)) * up).astype(jnp.bfloat16)
 
     def columns(i, of_col):
@@ -255,6 +282,7 @@
         return pl.ds(pl.multiple_of(start, CHUNK), CHUNK)
 
     def finish(i):
+        unit_copy(i).wait_recv()
         place_copy(i).wait_recv()
         ysend[i] = finished(i, 1 - col)
         out_ref[lax.div(i, per_expert), :, columns(i, col)] = finished(i, col)
@@ -284,6 +312,7 @@
 
     def last_loop(i, carry):
         core_copy(i).wait_send()
+        unit_copy(i).wait_send()
         place_copy(i).wait_send()
         col_copy(i).wait_send()
         return carry
@@ -305,8 +334,10 @@
         ((chunks, 2, 2, 2, SLOTS_DEV, CHUNK), f32),
         ((chunks, 2, 2, 2, SLOTS_DEV, CHUNK), f32),
         ((chunks, 2, 2, 2, SLOTS_DEV, CHUNK), f32),
-        ((chunks, 2, 2, SLOTS_DEV, CHUNK), f32),
-        ((chunks, 2, 2, SLOTS_DEV, CHUNK), f32),
+        ((chunks, 2, 2, SLOTS_DEV, CHUNK), jnp.int16),
+        ((chunks, 2, 2, SLOTS_DEV, CHUNK), jnp.int16),
+        ((chunks, 2, 8, CHUNK), f32),
+        ((chunks, 2, 8, CHUNK), f32),
         ((chunks, SLOTS_DEV, CHUNK), bf),
         ((chunks, SLOTS_DEV, CHUNK), bf),
     ]
@@ -355,7 +386,7 @@
         ]
         + [dma((2,))]
         + [ring_sems] * 4
-        + [dma((chunks,))] * 6,
+        + [dma((chunks,))] * 8,
         compiler_params=pltpu.CompilerParams(
             collective_id=0, has_side_effects=True, vmem_limit_bytes=VMEM_LIMIT
         ),

time: 118 us -> 92.6 us (0.78)
  Pallas kernels: 113 us -> 87.7 us
    pallas_call x1, Pallas kernels: 113 us -> 87.7 us  [fused_shards(): pl.pallas_call(functools.partial(kernel, n_row), out_shape=jax.ShapeDtype...]
where the time goes in v2:
time: 92.6 us; the launch traced here: 92.3 us
  Pallas kernels  87.7 us (95%)
  local copies, waits for them, and re-layouts  2.9 us (3%)
  other arithmetic  1.72 us (2%)
    pallas_call x1, Pallas kernels, fused_shards(): pl.pallas_call(functools.partial(kernel, n_row), out_shape=jax.ShapeDtype...  87.7 us
    unnamed x1, local copies, waits for them, and re-layouts  1.98 us

profile of v2, /device:TPU:0, one launch (start us, length us, event | category | flops | bytes accessed | tf_op | source)
XLA Modules:
  0.0 92.3 jit_solution(3556349318040370031)
XLA Ops:
  0.0 0.7 compare_reduce_fusion
  0.8 0.6 reduce-window.6
  1.4 0.2 slice_reduce_fusion
  1.5 0.2 reduce-window.9
  1.7 0.1 add_bitcast_fusion
  1.8 0.1 compare_select_fusion.2
  1.9 0.1 reshape.21
  2.0 0.6 copy.14
  2.7 87.7 %shard_map.46 = bf16[2,80,2048]{2,1,0:T(8,128)(2,1)} custom-call(bf16[4,80,1536]{2,1,0:T(8,128)(2,1)} %bitcast.23, s32[4,2,2,1,160]{4,3,2,1,0:T(1,128)} %bitcast.24, bf16[2,1536,1024]{2,1,0:T(8,128)(2,1)} %wg_hbm.1, bf16[2,1536,1024]{2,1,0:T(8,128)(2,1)} %wu_hbm.1), custom_call_target="tpu_custom_call" | custom-call | tf_op jit(solution)/shard_map/pallas_call | solution.py:374
  90.4 2.0 %copy.16 = bf16[2,80,2048]{2,1,0:T(8,128)(2,1)} copy(bf16[2,80,2048]{2,1,0:T(8,128)(2,1)} %shard_map.46) | data formatting | bytes 1310720
  (2 shorter events, 0.0 us)

commit v3 on v2

--- a/solution.py
+++ b/solution.py
@@ -9,7 +9,7 @@
 
 SLOTS_DEV = 80
 CHUNK = 256
-PIECE = 512
+PIECE = 256
 STEPS = 32767.0
 TINY = 1e-30
 MESH = pl.DeviceIdType.MESH
@@ -149,7 +149,7 @@
             device_id_type=MESH,
         )
 
-    def place_rows(ref, block, way, first):
+    def place_rows(ref, block, way, first, low, high):
         rows = ref[pl.ds(2 * way, 2)].reshape(2 * quarter, depth)
 
         def body(i, carry):
@@ -161,20 +161,21 @@
             slots[expert, side] = got if first else slots[expert, side] + got
             return carry
 
-        lax.fori_loop(0, 2 * experts, body, 0)
+        lax.fori_loop(2 * low, 2 * high, body, 0)
 
     for j in range(pieces):
         for way in range(2):
             ring(way, 1, j).start()
-    place_rows(tok_ref, row, 0, True)
-    place_rows(tok_ref, row, 1, False)
-
-    def settle(step):
-        for way in range(2):
-            for j in range(pieces):
-                across(way, step, j).wait_recv()
-            block = block_of(way, step)
-            place_rows(gath.at[block], block, way, False)
+    place_rows(tok_ref, row, 0, True, 0, experts)
+    place_rows(tok_ref, row, 1, False, 0, experts)
+
+    def arrived(step, way):
+        for j in range(pieces):
+            across(way, step, j).wait_recv()
+
+    def settle(step, way, low, high):
+        block = block_of(way, step)
+        place_rows(gath.at[block], block, way, False, low, high)
 
     for step in range(1, n_row):
         for j in range(pieces):
@@ -184,8 +185,9 @@
                     ring(way, step + 1, j).start()
                 across(way, step, j).start()
         if step > 1:
-            settle(step - 1)
-    settle(n_row - 1)
+            for way in range(2):
+                arrived(step - 1, way)
+                settle(step - 1, way, 0, experts)
 
     for copy in w_copies:
         copy.wait()
@@ -264,7 +266,12 @@
 
         return carry
 
-    lax.fori_loop(0, chunks, first_loop, 0)
+    for expert in range(experts):
+        for way in range(2):
+            if expert == 0:
+                arrived(n_row - 1, way)
+            settle(n_row - 1, way, expert, expert + 1)
+        lax.fori_loop(expert * per_expert, (expert + 1) * per_expert, first_loop, 0)
     pass_on(chunks - 1)
 
     def finished(i, side):

time: 92.6 us -> 91.9 us (level)
  no operation moved by 1% of the time
where the time goes in v3:
time: 91.9 us; the launch traced here: 91.7 us
  Pallas kernels  87 us (95%)
  local copies, waits for them, and re-layouts  2.9 us (3%)
  other arithmetic  1.72 us (2%)
    pallas_call x1, Pallas kernels, fused_shards(): pl.pallas_call(functools.partial(kernel, n_row), out_shape=jax.ShapeDtype...  87 us
    unnamed x1, local copies, waits for them, and re-layouts  1.98 us

profile of v3, /device:TPU:0, one launch (start us, length us, event | category | flops | bytes accessed | tf_op | source)
XLA Modules:
  0.0 91.7 jit_solution(12510478606091662526)
XLA Ops:
  0.0 0.7 compare_reduce_fusion
  0.8 0.6 reduce-window.6
  1.4 0.2 slice_reduce_fusion
  1.5 0.2 reduce-window.9
  1.7 0.1 add_bitcast_fusion
  1.8 0.1 compare_select_fusion.2
  1.9 0.1 reshape.21
  2.0 0.6 copy.14
  2.7 87.0 %shard_map.46 = bf16[2,80,2048]{2,1,0:T(8,128)(2,1)} custom-call(bf16[4,80,1536]{2,1,0:T(8,128)(2,1)} %bitcast.23, s32[4,2,2,1,160]{4,3,2,1,0:T(1,128)} %bitcast.24, bf16[2,1536,1024]{2,1,0:T(8,128)(2,1)} %wg_hbm.1, bf16[2,1536,1024]{2,1,0:T(8,128)(2,1)} %wu_hbm.1), custom_call_target="tpu_custom_call" | custom-call | tf_op jit(solution)/shard_map/pallas_call | solution.py:381
  89.7 2.0 %copy.16 = bf16[2,80,2048]{2,1,0:T(8,128)(2,1)} copy(bf16[2,80,2048]{2,1,0:T(8,128)(2,1)} %shard_map.46) | data formatting | bytes 1310720
  (2 shorter events, 0.0 us)
